TPU v7x, 32 devices: a whole 2x2x4 slice. The times are simulated.
32 devices in a mesh: rows: 2 (over core), cols: 4 (over y, x), slabs: 4 (over z).
Axes of the slice: x: 2, y: 2, z: 4, core: 2. Of those that a mesh axis runs over, the one named last changes fastest.
Arguments:
- tracer: float32 [8, 256, 384, 128], P('rows', 'cols', 'slabs'), may hold values from 0.2 to 1.8
- crowding: float32 [8, 256, 384, 128], P('rows', 'cols', 'slabs'), may hold values from 0.5 to 2
Outputs:
- tracer_end: float32 [8, 256, 384, 128], P('rows', 'cols', 'slabs')
All inputs are finite; a program needn't handle non-finite values.
Results may differ from a plain program's by a relative error of at most 0.00002.
Values sent between devices are 32-bit elements.
A program may use at most 448 MiB of HBM per device.

v0:
```python
import jax
import jax.numpy as jnp
from jax import lax
from jax.sharding import PartitionSpec as P

STEPS = 4


def with_halo(block, sides, width):
    for axis, dim in sides:
        count = lax.axis_size(axis)
        forward = [(i, i + 1) for i in range(count - 1)]
        backward = [(target, source) for source, target in forward]
        low = lax.ppermute(
            lax.slice_in_dim(block, block.shape[dim] - width, None, axis=dim), axis, forward
        )
        high = lax.ppermute(lax.slice_in_dim(block, 0, width, axis=dim), axis, backward)
        block = jnp.concatenate([low, block, high], axis=dim)
    return block


def inner_cells(values, dims):
    for dim in dims:
        values = lax.slice_in_dim(values, 1, values.shape[dim] - 1, axis=dim)
    return values


def side_cells(values, dim, start, dims):
    others = [other for other in dims if other != dim]
    values = inner_cells(values, others)
    return lax.slice_in_dim(values, start, start + values.shape[dim] - 2, axis=dim)


def advance(padded, crowding):
    middle = inner_cells(padded, (0, 1, 2))
    lower = [side_cells(padded, dim, 0, (0, 1, 2)) for dim in (0, 1, 2)]
    upper = [side_cells(padded, dim, 2, (0, 1, 2)) for dim in (0, 1, 2)]
    spread = lower[0] + upper[0] + lower[1] + upper[1] + lower[2] + upper[2] - 6.0 * middle
    return middle + 0.1 * spread + 0.2 * middle * (1.0 - middle * crowding)


def on_device(tracer, crowding):
    for step in range(STEPS):
        padded = with_halo(tracer, (("rows", 0), ("cols", 1), ("slabs", 2)), 1)
        tracer = advance(padded, crowding)
    return tracer


def solution(mesh):
    placed = (P("rows", "cols", "slabs", None), P("rows", "cols", "slabs", None))
    return jax.shard_map(
        on_device,
        mesh=mesh,
        in_specs=placed,
        out_specs=P("rows", "cols", "slabs", None),
        check_vma=False,
    )
```

profile of v0, /device:TPU:0, one launch (start us, length us, event | category | flops | bytes accessed | tf_op | source)
XLA Modules:
  0.0 361.2 jit_solution(10264535121621644159)
XLA Ops:
  0.0 5.0 %fusion.40 = (f32[1,64,96,128]{3,2,1,0:T(8,128)}, f32[1,64,96,128]{3,2,1,0:T(8,128)S(1)}) fusion(f32[4,64,96,128]{3,2,1,0:T(8,128)} %param.2), kind=kLoop, calls=%fused_computation.134 | loop fusion | bytes 12582912 | tf_op jit(solution)/shard_map/slice | solution.py:17
  5.0 2.6 collective-permute-start
  7.5 1.3 collective-permute-start.1
  8.8 3.8 %collective-permute-done = f32[1,64,96,128]{3,2,1,0:T(8,128)S(1)} collective-permute-done((f32[1,64,96,128]{3,2,1,0:T(8,128)S(1)}, f32[1,64,96,128]{3,2,1,0:T(8,128)S(1)}, u32[]{:S(2)}, u32[]{:S(2)}) %collective-permute-start) | collective-permute-done | bytes 3145760 | tf_op jit(solution)/shard_map/ppermute | solution.py:14
  12.6 1.9 constant_dynamic-update-slice_fusion.2
  14.5 10.3 %constant_dynamic-update-slice_fusion.1 = f32[6,64,96,128]{3,2,1,0:T(8,128)} fusion(f32[6,64,96,128]{3,2,1,0:T(8,128)} %constant_dynamic-update-slice_fusion.2, f32[4,64,96,128]{3,2,1,0:T(8,128)} %param.2), kind=kLoop, calls=%fused_computation.128 | loop fusion | bytes 25165824
  24.8 2.0 constant_dynamic-update-slice_fusion
  26.8 1.2 fusion.36
  28.0 4.2 %collective-permute-start.2 = (f32[6,1,96,128]{3,2,1,0:T(8,128)S(1)}, f32[6,1,96,128]{3,2,1,0:T(8,128)S(1)}, u32[]{:S(2)}, u32[]{:S(2)}) collective-permute-start(f32[6,1,96,128]{3,2,1,0:T(8,128)S(1)} %get-tuple-element.19), channel_id=1, source_target_pairs={{0,4},{4,8},{8,12},{1,5},{5,9},{9,13},{2,6},{6,10},{10,14},{3,7},{... | collective-permute-start | bytes 884744 | tf_op jit(solution)/shard_map/ppermute | solution.py:14
  32.2 1.3 collective-permute-start.3
  33.5 5.5 %collective-permute-done.2 = f32[6,1,96,128]{3,2,1,0:T(8,128)S(1)} collective-permute-done((f32[6,1,96,128]{3,2,1,0:T(8,128)S(1)}, f32[6,1,96,128]{3,2,1,0:T(8,128)S(1)}, u32[]{:S(2)}, u32[]{:S(2)}) %collective-permute-start.2) | collective-permute-done | bytes 294944 | tf_op jit(solution)/shard_map/ppermute | solution.py:14
  39.0 8.3 %collective-permute-done.3 = f32[6,1,96,128]{3,2,1,0:T(8,128)S(1)} collective-permute-done((f32[6,1,96,128]{3,2,1,0:T(8,128)S(1)}, f32[6,1,96,128]{3,2,1,0:T(8,128)S(1)}, u32[]{:S(2)}, u32[]{:S(2)}) %collective-permute-start.3) | collective-permute-done | bytes 294944 | tf_op jit(solution)/shard_map/ppermute | solution.py:17
  47.2 2.3 pad_maximum_fusion.90
  49.6 1.3 collective-permute-start.5
  50.9 4.6 %collective-permute-start.4 = (f32[6,66,1,128]{3,1,2,0:T(8,128)S(1)}, f32[6,66,1,128]{3,1,2,0:T(8,128)S(1)}, u32[]{:S(2)}, u32[]{:S(2)}) collective-permute-start(f32[6,66,1,128]{3,1,2,0:T(8,128)S(1)} %copy.17), channel_id=1, source_target_pairs={{0,1},{1,2},{2,3},{4,5},{5,6},{6,7},{8,9},{9,10},{10,11},{12,13},{... | collective-permute-start | bytes 608264 | tf_op jit(solution)/shard_map/ppermute | solution.py:14
  55.5 2.9 collective-permute-done.5
  58.3 0.9 copy.20
  59.6 0.9 copy.18
  60.4 42.2 %fusion.31 = f32[4,64,96,128]{3,2,1,0:T(8,128)} fusion(f32[4,64,96,128]{3,2,1,0:T(8,128)} %param.2, f32[6,66,1,128]{3,2,1,0:T(1,128)} %copy.20, f32[6,1,96,128]{3,2,1,0:T(8,128)} %copy-done.7, f32[6,64,96,128]{3,2,1,0:T(8,128)} %constant_dynamic-update-slice_fusion, f32[6,1,96,128]{3,2,1,0:T(8,128)S(1)} %collective-permute-done.2, ...), kind=kLoop, calls=%fused_computation.86 | loop fusion | flops 75497472 | bytes 63909888 | tf_op jit(solution)/shard_map/add | solution.py:39
  102.7 3.4 fusion.39
  106.1 1.8 collective-permute-start.6
  107.9 1.4 collective-permute-start.7
  109.3 3.6 %collective-permute-done.6 = f32[1,64,96,128]{3,2,1,0:T(8,128)S(1)} collective-permute-done((f32[1,64,96,128]{3,2,1,0:T(8,128)S(1)}, f32[1,64,96,128]{3,2,1,0:T(8,128)S(1)}, u32[]{:S(2)}, u32[]{:S(2)}) %collective-permute-start.6) | collective-permute-done | bytes 3145760 | tf_op jit(solution)/shard_map/ppermute | solution.py:14
  113.0 2.6 collective-permute-done.7
  115.6 3.4 collective-permute-start.8
  119.1 1.3 collective-permute-start.9
  120.4 5.2 %collective-permute-done.8 = f32[6,1,96,128]{3,2,1,0:T(8,128)S(1)} collective-permute-done((f32[6,1,96,128]{3,2,1,0:T(8,128)S(1)}, f32[6,1,96,128]{3,2,1,0:T(8,128)S(1)}, u32[]{:S(2)}, u32[]{:S(2)}) %collective-permute-start.8) | collective-permute-done | bytes 294944 | tf_op jit(solution)/shard_map/ppermute | solution.py:14
  125.6 7.1 %collective-permute-done.9 = f32[6,1,96,128]{3,2,1,0:T(8,128)S(1)} collective-permute-done((f32[6,1,96,128]{3,2,1,0:T(8,128)S(1)}, f32[6,1,96,128]{3,2,1,0:T(8,128)S(1)}, u32[]{:S(2)}, u32[]{:S(2)}) %collective-permute-start.9) | collective-permute-done | bytes 294944 | tf_op jit(solution)/shard_map/ppermute | solution.py:17
  133.4 1.3 collective-permute-start.11
  134.7 5.2 %collective-permute-start.10 = (f32[6,66,1,128]{3,1,2,0:T(8,128)S(1)}, f32[6,66,1,128]{3,1,2,0:T(8,128)S(1)}, u32[]{:S(2)}, u32[]{:S(2)}) collective-permute-start(f32[6,66,1,128]{3,1,2,0:T(8,128)S(1)} %copy.21), channel_id=1, source_target_pairs={{0,1},{1,2},{2,3},{4,5},{5,6},{6,7},{8,9},{9,10},{10,11},{12,13},{... | collective-permute-start | bytes 608264 | tf_op jit(solution)/shard_map/ppermute | solution.py:14
  139.9 3.0 collective-permute-done.11
  142.9 0.9 copy.24
  144.2 0.9 copy.22
  145.0 45.2 %fusion.22 = f32[4,64,96,128]{3,2,1,0:T(8,128)} fusion(f32[4,64,96,128]{3,2,1,0:T(8,128)} %fusion.31, f32[6,66,1,128]{3,2,1,0:T(1,128)} %copy.24, f32[6,1,96,128]{3,2,1,0:T(8,128)} %copy-done.8, f32[6,1,96,128]{3,2,1,0:T(8,128)S(1)} %collective-permute-done.8, f32[1,64,96,128]{3,2,1,0:T(8,128)} %copy-done.3, ...), kind=kLoop, calls=%fused_computation.59 | loop fusion | flops 100663296 | bytes 45035520 | tf_op jit(solution)/shard_map/add | solution.py:39
  190.2 3.4 fusion.38
  193.7 1.8 collective-permute-start.12
  195.4 1.4 collective-permute-start.13
  196.9 3.6 %collective-permute-done.12 = f32[1,64,96,128]{3,2,1,0:T(8,128)S(1)} collective-permute-done((f32[1,64,96,128]{3,2,1,0:T(8,128)S(1)}, f32[1,64,96,128]{3,2,1,0:T(8,128)S(1)}, u32[]{:S(2)}, u32[]{:S(2)}) %collective-permute-start.12) | collective-permute-done | bytes 3145760 | tf_op jit(solution)/shard_map/ppermute | solution.py:14
  200.5 2.6 collective-permute-done.13
  203.2 1.5 collective-permute-start.14
  204.7 1.3 collective-permute-start.15
  206.0 5.4 %collective-permute-done.14 = f32[6,1,96,128]{3,2,1,0:T(8,128)S(1)} collective-permute-done((f32[6,1,96,128]{3,2,1,0:T(8,128)S(1)}, f32[6,1,96,128]{3,2,1,0:T(8,128)S(1)}, u32[]{:S(2)}, u32[]{:S(2)}) %collective-permute-start.14) | collective-permute-done | bytes 294944 | tf_op jit(solution)/shard_map/ppermute | solution.py:14
  211.3 6.9 %collective-permute-done.15 = f32[6,1,96,128]{3,2,1,0:T(8,128)S(1)} collective-permute-done((f32[6,1,96,128]{3,2,1,0:T(8,128)S(1)}, f32[6,1,96,128]{3,2,1,0:T(8,128)S(1)}, u32[]{:S(2)}, u32[]{:S(2)}) %collective-permute-start.15) | collective-permute-done | bytes 294944 | tf_op jit(solution)/shard_map/ppermute | solution.py:17
  219.0 1.3 collective-permute-start.17
  220.3 5.0 %collective-permute-start.16 = (f32[6,66,1,128]{3,1,2,0:T(8,128)S(1)}, f32[6,66,1,128]{3,1,2,0:T(8,128)S(1)}, u32[]{:S(2)}, u32[]{:S(2)}) collective-permute-start(f32[6,66,1,128]{3,1,2,0:T(8,128)S(1)} %copy.25), channel_id=1, source_target_pairs={{0,1},{1,2},{2,3},{4,5},{5,6},{6,7},{8,9},{9,10},{10,11},{12,13},{... | collective-permute-start | bytes 608264 | tf_op jit(solution)/shard_map/ppermute | solution.py:14
  225.4 3.2 collective-permute-done.17
  228.6 0.9 copy.28
  229.8 0.9 copy.26
  230.6 44.5 %fusion.13 = f32[4,64,96,128]{3,2,1,0:T(8,128)} fusion(f32[4,64,96,128]{3,2,1,0:T(8,128)} %fusion.22, f32[6,66,1,128]{3,2,1,0:T(1,128)} %copy.28, f32[6,1,96,128]{3,2,1,0:T(8,128)} %copy-done.9, f32[6,1,96,128]{3,2,1,0:T(8,128)S(1)} %collective-permute-done.14, f32[1,64,96,128]{3,2,1,0:T(8,128)} %copy-done.4, ...), kind=kLoop, calls=%fused_computation.32 | loop fusion | flops 100663296 | bytes 45035520 | tf_op jit(solution)/shard_map/add | solution.py:39
  275.2 3.4 fusion.37
  278.6 1.8 collective-permute-start.18
  280.4 1.6 collective-permute-start.19
  282.0 3.4 collective-permute-done.18
  285.4 2.6 collective-permute-done.19
  288.1 1.5 collective-permute-start.20
  289.6 1.3 collective-permute-start.21
  290.9 5.4 %collective-permute-done.20 = f32[6,1,96,128]{3,2,1,0:T(8,128)S(1)} collective-permute-done((f32[6,1,96,128]{3,2,1,0:T(8,128)S(1)}, f32[6,1,96,128]{3,2,1,0:T(8,128)S(1)}, u32[]{:S(2)}, u32[]{:S(2)}) %collective-permute-start.20) | collective-permute-done | bytes 294944 | tf_op jit(solution)/shard_map/ppermute | solution.py:14
  296.2 6.9 %collective-permute-done.21 = f32[6,1,96,128]{3,2,1,0:T(8,128)S(1)} collective-permute-done((f32[6,1,96,128]{3,2,1,0:T(8,128)S(1)}, f32[6,1,96,128]{3,2,1,0:T(8,128)S(1)}, u32[]{:S(2)}, u32[]{:S(2)}) %collective-permute-start.21) | collective-permute-done | bytes 294944 | tf_op jit(solution)/shard_map/ppermute | solution.py:17
  303.9 1.3 collective-permute-start.23
  305.3 5.0 %collective-permute-start.22 = (f32[6,66,1,128]{3,1,2,0:T(8,128)S(1)}, f32[6,66,1,128]{3,1,2,0:T(8,128)S(1)}, u32[]{:S(2)}, u32[]{:S(2)}) collective-permute-start(f32[6,66,1,128]{3,1,2,0:T(8,128)S(1)} %copy.29), channel_id=1, source_target_pairs={{0,1},{1,2},{2,3},{4,5},{5,6},{6,7},{8,9},{9,10},{10,11},{12,13},{... | collective-permute-start | bytes 608264 | tf_op jit(solution)/shard_map/ppermute | solution.py:14
  310.3 3.2 collective-permute-done.23
  313.5 0.9 copy.32
  314.7 0.9 copy.30
  315.6 45.4 %fusion.4 = f32[4,64,96,128]{3,2,1,0:T(8,128)} fusion(f32[4,64,96,128]{3,2,1,0:T(8,128)} %fusion.13, f32[6,66,1,128]{3,2,1,0:T(1,128)} %copy.32, f32[6,1,96,128]{3,2,1,0:T(8,128)} %copy-done.10, f32[6,1,96,128]{3,2,1,0:T(8,128)S(1)} %collective-permute-done.20, f32[1,64,96,128]{3,2,1,0:T(8,128)} %copy-done.5, ...), kind=kLoop, calls=%fused_computation.5 | loop fusion | flops 100663296 | bytes 45035520 | tf_op jit(solution)/shard_map/add | solution.py:39
  (41 shorter events, 3.7 us)
Async XLA Ops:
  5.0 7.7 %collective-permute-start = (f32[1,64,96,128]{3,2,1,0:T(8,128)S(1)}, f32[1,64,96,128]{3,2,1,0:T(8,128)S(1)}, u32[]{:S(2)}, u32[]{:S(2)}) collective-permute-start(f32[1,64,96,128]{3,2,1,0:T(8,128)S(1)} %get-tuple-element.28), channel_id=1, source_target_pairs={{0,16},{1,17},{2,18},{3,19},{4,20},{5,21},{6,22},{7,23},{8,24},{9,... | collective-permute-start | bytes 9437192 | tf_op jit(solution)/shard_map/ppermute | solution.py:14
  7.5 17.2 %collective-permute-start.1 = (f32[1,64,96,128]{3,2,1,0:T(8,128)}, f32[1,64,96,128]{3,2,1,0:T(8,128)S(1)}, u32[]{:S(2)}, u32[]{:S(2)}) collective-permute-start(f32[1,64,96,128]{3,2,1,0:T(8,128)} %get-tuple-element.27), channel_id=1, source_target_pairs={{16,0},{17,1},{18,2},{19,3},{20,4},{21,5},{22,6},{23,7},{24,8},{25... | collective-permute-start | bytes 9437192 | tf_op jit(solution)/shard_map/ppermute | solution.py:17
  24.8 24.8 %copy-start.6 = (f32[1,64,96,128]{3,2,1,0:T(8,128)}, f32[1,64,96,128]{3,2,1,0:T(8,128)S(1)}, u32[]{:S(2)}) copy-start(f32[1,64,96,128]{3,2,1,0:T(8,128)S(1)} %collective-permute-done.1) | copy-start | bytes 9437188
  28.0 11.0 %collective-permute-start.2 = (f32[6,1,96,128]{3,2,1,0:T(8,128)S(1)}, f32[6,1,96,128]{3,2,1,0:T(8,128)S(1)}, u32[]{:S(2)}, u32[]{:S(2)}) collective-permute-start(f32[6,1,96,128]{3,2,1,0:T(8,128)S(1)} %get-tuple-element.19), channel_id=1, source_target_pairs={{0,4},{4,8},{8,12},{1,5},{5,9},{9,13},{2,6},{6,10},{10,14},{3,7},{... | collective-permute-start | bytes 884744 | tf_op jit(solution)/shard_map/ppermute | solution.py:14
  32.2 15.0 %collective-permute-start.3 = (f32[6,1,96,128]{3,2,1,0:T(8,128)S(1)}, f32[6,1,96,128]{3,2,1,0:T(8,128)S(1)}, u32[]{:S(2)}, u32[]{:S(2)}) collective-permute-start(f32[6,1,96,128]{3,2,1,0:T(8,128)S(1)} %get-tuple-element.20), channel_id=1, source_target_pairs={{4,0},{8,4},{12,8},{5,1},{9,5},{13,9},{6,2},{10,6},{14,10},{7,3},{... | collective-permute-start | bytes 884744 | tf_op jit(solution)/shard_map/ppermute | solution.py:17
  47.2 2.3 copy-start.7
  49.6 8.7 %collective-permute-start.5 = (f32[6,66,1,128]{3,1,2,0:T(8,128)S(1)}, f32[6,66,1,128]{3,1,2,0:T(8,128)S(1)}, u32[]{:S(2)}, u32[]{:S(2)}) collective-permute-start(f32[6,66,1,128]{3,1,2,0:T(8,128)S(1)} %copy.19), channel_id=1, source_target_pairs={{1,0},{2,1},{3,2},{5,4},{6,5},{7,6},{9,8},{10,9},{11,10},{13,12},{... | collective-permute-start | bytes 608264 | tf_op jit(solution)/shard_map/ppermute | solution.py:17
  50.9 8.6 %collective-permute-start.4 = (f32[6,66,1,128]{3,1,2,0:T(8,128)S(1)}, f32[6,66,1,128]{3,1,2,0:T(8,128)S(1)}, u32[]{:S(2)}, u32[]{:S(2)}) collective-permute-start(f32[6,66,1,128]{3,1,2,0:T(8,128)S(1)} %copy.17), channel_id=1, source_target_pairs={{0,1},{1,2},{2,3},{4,5},{5,6},{6,7},{8,9},{9,10},{10,11},{12,13},{... | collective-permute-start | bytes 608264 | tf_op jit(solution)/shard_map/ppermute | solution.py:14
  102.7 12.9 %copy-start = (f32[4,64,96,128]{3,2,1,0:T(8,128)S(1)}, f32[4,64,96,128]{3,2,1,0:T(8,128)}, u32[]{:S(2)}) copy-start(f32[4,64,96,128]{3,2,1,0:T(8,128)} %fusion.31) | copy-start | bytes 37748740
  106.1 6.8 %collective-permute-start.6 = (f32[1,64,96,128]{3,2,1,0:T(8,128)S(1)}, f32[1,64,96,128]{3,2,1,0:T(8,128)S(1)}, u32[]{:S(2)}, u32[]{:S(2)}) collective-permute-start(f32[1,64,96,128]{3,2,1,0:T(8,128)S(1)} %get-tuple-element.25), channel_id=1, source_target_pairs={{0,16},{1,17},{2,18},{3,19},{4,20},{5,21},{6,22},{7,23},{8,24},{9,... | collective-permute-start | bytes 9437192 | tf_op jit(solution)/shard_map/ppermute | solution.py:14
  107.9 7.7 %collective-permute-start.7 = (f32[1,64,96,128]{3,2,1,0:T(8,128)S(1)}, f32[1,64,96,128]{3,2,1,0:T(8,128)S(1)}, u32[]{:S(2)}, u32[]{:S(2)}) collective-permute-start(f32[1,64,96,128]{3,2,1,0:T(8,128)S(1)} %get-tuple-element.26), channel_id=1, source_target_pairs={{16,0},{17,1},{18,2},{19,3},{20,4},{21,5},{22,6},{23,7},{24,8},{25... | collective-permute-start | bytes 9437192 | tf_op jit(solution)/shard_map/ppermute | solution.py:17
  115.6 17.4 %copy-start.3 = (f32[1,64,96,128]{3,2,1,0:T(8,128)}, f32[1,64,96,128]{3,2,1,0:T(8,128)S(1)}, u32[]{:S(2)}) copy-start(f32[1,64,96,128]{3,2,1,0:T(8,128)S(1)} %collective-permute-done.7) | copy-start | bytes 9437188
  115.6 10.0 %collective-permute-start.8 = (f32[6,1,96,128]{3,2,1,0:T(8,128)S(1)}, f32[6,1,96,128]{3,2,1,0:T(8,128)S(1)}, u32[]{:S(2)}, u32[]{:S(2)}) collective-permute-start(f32[6,1,96,128]{3,2,1,0:T(8,128)S(1)} %get-tuple-element.17), channel_id=1, source_target_pairs={{0,4},{4,8},{8,12},{1,5},{5,9},{9,13},{2,6},{6,10},{10,14},{3,7},{... | collective-permute-start | bytes 884744 | tf_op jit(solution)/shard_map/ppermute | solution.py:14
  119.1 13.6 %collective-permute-start.9 = (f32[6,1,96,128]{3,2,1,0:T(8,128)S(1)}, f32[6,1,96,128]{3,2,1,0:T(8,128)S(1)}, u32[]{:S(2)}, u32[]{:S(2)}) collective-permute-start(f32[6,1,96,128]{3,2,1,0:T(8,128)S(1)} %get-tuple-element.18), channel_id=1, source_target_pairs={{4,0},{8,4},{12,8},{5,1},{9,5},{13,9},{6,2},{10,6},{14,10},{7,3},{... | collective-permute-start | bytes 884744 | tf_op jit(solution)/shard_map/ppermute | solution.py:17
  132.7 0.7 copy-start.8
  133.4 9.5 %collective-permute-start.11 = (f32[6,66,1,128]{3,1,2,0:T(8,128)S(1)}, f32[6,66,1,128]{3,1,2,0:T(8,128)S(1)}, u32[]{:S(2)}, u32[]{:S(2)}) collective-permute-start(f32[6,66,1,128]{3,1,2,0:T(8,128)S(1)} %copy.23), channel_id=1, source_target_pairs={{1,0},{2,1},{3,2},{5,4},{6,5},{7,6},{9,8},{10,9},{11,10},{13,12},{... | collective-permute-start | bytes 608264 | tf_op jit(solution)/shard_map/ppermute | solution.py:17
  134.7 9.4 %collective-permute-start.10 = (f32[6,66,1,128]{3,1,2,0:T(8,128)S(1)}, f32[6,66,1,128]{3,1,2,0:T(8,128)S(1)}, u32[]{:S(2)}, u32[]{:S(2)}) collective-permute-start(f32[6,66,1,128]{3,1,2,0:T(8,128)S(1)} %copy.21), channel_id=1, source_target_pairs={{0,1},{1,2},{2,3},{4,5},{5,6},{6,7},{8,9},{9,10},{10,11},{12,13},{... | collective-permute-start | bytes 608264 | tf_op jit(solution)/shard_map/ppermute | solution.py:14
  190.2 12.9 %copy-start.1 = (f32[4,64,96,128]{3,2,1,0:T(8,128)S(1)}, f32[4,64,96,128]{3,2,1,0:T(8,128)}, u32[]{:S(2)}) copy-start(f32[4,64,96,128]{3,2,1,0:T(8,128)} %fusion.22) | copy-start | bytes 37748740
  193.7 6.8 %collective-permute-start.12 = (f32[1,64,96,128]{3,2,1,0:T(8,128)S(1)}, f32[1,64,96,128]{3,2,1,0:T(8,128)S(1)}, u32[]{:S(2)}, u32[]{:S(2)}) collective-permute-start(f32[1,64,96,128]{3,2,1,0:T(8,128)S(1)} %get-tuple-element.23), channel_id=1, source_target_pairs={{0,16},{1,17},{2,18},{3,19},{4,20},{5,21},{6,22},{7,23},{8,24},{9,... | collective-permute-start | bytes 9437192 | tf_op jit(solution)/shard_map/ppermute | solution.py:14
  195.4 7.7 %collective-permute-start.13 = (f32[1,64,96,128]{3,2,1,0:T(8,128)S(1)}, f32[1,64,96,128]{3,2,1,0:T(8,128)S(1)}, u32[]{:S(2)}, u32[]{:S(2)}) collective-permute-start(f32[1,64,96,128]{3,2,1,0:T(8,128)S(1)} %get-tuple-element.24), channel_id=1, source_target_pairs={{16,0},{17,1},{18,2},{19,3},{20,4},{21,5},{22,6},{23,7},{24,8},{25... | collective-permute-start | bytes 9437192 | tf_op jit(solution)/shard_map/ppermute | solution.py:17
  203.1 15.4 %copy-start.4 = (f32[1,64,96,128]{3,2,1,0:T(8,128)}, f32[1,64,96,128]{3,2,1,0:T(8,128)S(1)}, u32[]{:S(2)}) copy-start(f32[1,64,96,128]{3,2,1,0:T(8,128)S(1)} %collective-permute-done.13) | copy-start | bytes 9437188
  203.2 8.1 %collective-permute-start.14 = (f32[6,1,96,128]{3,2,1,0:T(8,128)S(1)}, f32[6,1,96,128]{3,2,1,0:T(8,128)S(1)}, u32[]{:S(2)}, u32[]{:S(2)}) collective-permute-start(f32[6,1,96,128]{3,2,1,0:T(8,128)S(1)} %get-tuple-element.15), channel_id=1, source_target_pairs={{0,4},{4,8},{8,12},{1,5},{5,9},{9,13},{2,6},{6,10},{10,14},{3,7},{... | collective-permute-start | bytes 884744 | tf_op jit(solution)/shard_map/ppermute | solution.py:14
  204.7 13.6 %collective-permute-start.15 = (f32[6,1,96,128]{3,2,1,0:T(8,128)S(1)}, f32[6,1,96,128]{3,2,1,0:T(8,128)S(1)}, u32[]{:S(2)}, u32[]{:S(2)}) collective-permute-start(f32[6,1,96,128]{3,2,1,0:T(8,128)S(1)} %get-tuple-element.16), channel_id=1, source_target_pairs={{4,0},{8,4},{12,8},{5,1},{9,5},{13,9},{6,2},{10,6},{14,10},{7,3},{... | collective-permute-start | bytes 884744 | tf_op jit(solution)/shard_map/ppermute | solution.py:17
  218.3 0.7 copy-start.9
  219.0 9.5 %collective-permute-start.17 = (f32[6,66,1,128]{3,1,2,0:T(8,128)S(1)}, f32[6,66,1,128]{3,1,2,0:T(8,128)S(1)}, u32[]{:S(2)}, u32[]{:S(2)}) collective-permute-start(f32[6,66,1,128]{3,1,2,0:T(8,128)S(1)} %copy.27), channel_id=1, source_target_pairs={{1,0},{2,1},{3,2},{5,4},{6,5},{7,6},{9,8},{10,9},{11,10},{13,12},{... | collective-permute-start | bytes 608264 | tf_op jit(solution)/shard_map/ppermute | solution.py:17
  220.3 9.4 %collective-permute-start.16 = (f32[6,66,1,128]{3,1,2,0:T(8,128)S(1)}, f32[6,66,1,128]{3,1,2,0:T(8,128)S(1)}, u32[]{:S(2)}, u32[]{:S(2)}) collective-permute-start(f32[6,66,1,128]{3,1,2,0:T(8,128)S(1)} %copy.25), channel_id=1, source_target_pairs={{0,1},{1,2},{2,3},{4,5},{5,6},{6,7},{8,9},{9,10},{10,11},{12,13},{... | collective-permute-start | bytes 608264 | tf_op jit(solution)/shard_map/ppermute | solution.py:14
  275.1 12.9 %copy-start.2 = (f32[4,64,96,128]{3,2,1,0:T(8,128)S(1)}, f32[4,64,96,128]{3,2,1,0:T(8,128)}, u32[]{:S(2)}) copy-start(f32[4,64,96,128]{3,2,1,0:T(8,128)} %fusion.13) | copy-start | bytes 37748740
  278.6 6.8 %collective-permute-start.18 = (f32[1,64,96,128]{3,2,1,0:T(8,128)S(1)}, f32[1,64,96,128]{3,2,1,0:T(8,128)S(1)}, u32[]{:S(2)}, u32[]{:S(2)}) collective-permute-start(f32[1,64,96,128]{3,2,1,0:T(8,128)S(1)} %get-tuple-element.21), channel_id=1, source_target_pairs={{0,16},{1,17},{2,18},{3,19},{4,20},{5,21},{6,22},{7,23},{8,24},{9,... | collective-permute-start | bytes 9437192 | tf_op jit(solution)/shard_map/ppermute | solution.py:14
  280.4 7.7 %collective-permute-start.19 = (f32[1,64,96,128]{3,2,1,0:T(8,128)S(1)}, f32[1,64,96,128]{3,2,1,0:T(8,128)S(1)}, u32[]{:S(2)}, u32[]{:S(2)}) collective-permute-start(f32[1,64,96,128]{3,2,1,0:T(8,128)S(1)} %get-tuple-element.22), channel_id=1, source_target_pairs={{16,0},{17,1},{18,2},{19,3},{20,4},{21,5},{22,6},{23,7},{24,8},{25... | collective-permute-start | bytes 9437192 | tf_op jit(solution)/shard_map/ppermute | solution.py:17
  288.1 15.4 %copy-start.5 = (f32[1,64,96,128]{3,2,1,0:T(8,128)}, f32[1,64,96,128]{3,2,1,0:T(8,128)S(1)}, u32[]{:S(2)}) copy-start(f32[1,64,96,128]{3,2,1,0:T(8,128)S(1)} %collective-permute-done.19) | copy-start | bytes 9437188
  288.1 8.1 %collective-permute-start.20 = (f32[6,1,96,128]{3,2,1,0:T(8,128)S(1)}, f32[6,1,96,128]{3,2,1,0:T(8,128)S(1)}, u32[]{:S(2)}, u32[]{:S(2)}) collective-permute-start(f32[6,1,96,128]{3,2,1,0:T(8,128)S(1)} %get-tuple-element.13), channel_id=1, source_target_pairs={{0,4},{4,8},{8,12},{1,5},{5,9},{9,13},{2,6},{6,10},{10,14},{3,7},{... | collective-permute-start | bytes 884744 | tf_op jit(solution)/shard_map/ppermute | solution.py:14
  289.6 13.6 %collective-permute-start.21 = (f32[6,1,96,128]{3,2,1,0:T(8,128)S(1)}, f32[6,1,96,128]{3,2,1,0:T(8,128)S(1)}, u32[]{:S(2)}, u32[]{:S(2)}) collective-permute-start(f32[6,1,96,128]{3,2,1,0:T(8,128)S(1)} %get-tuple-element.14), channel_id=1, source_target_pairs={{4,0},{8,4},{12,8},{5,1},{9,5},{13,9},{6,2},{10,6},{14,10},{7,3},{... | collective-permute-start | bytes 884744 | tf_op jit(solution)/shard_map/ppermute | solution.py:17
  303.2 0.7 copy-start.10
  303.9 9.5 %collective-permute-start.23 = (f32[6,66,1,128]{3,1,2,0:T(8,128)S(1)}, f32[6,66,1,128]{3,1,2,0:T(8,128)S(1)}, u32[]{:S(2)}, u32[]{:S(2)}) collective-permute-start(f32[6,66,1,128]{3,1,2,0:T(8,128)S(1)} %copy.31), channel_id=1, source_target_pairs={{1,0},{2,1},{3,2},{5,4},{6,5},{7,6},{9,8},{10,9},{11,10},{13,12},{... | collective-permute-start | bytes 608264 | tf_op jit(solution)/shard_map/ppermute | solution.py:17
  305.3 9.4 %collective-permute-start.22 = (f32[6,66,1,128]{3,1,2,0:T(8,128)S(1)}, f32[6,66,1,128]{3,1,2,0:T(8,128)S(1)}, u32[]{:S(2)}, u32[]{:S(2)}) collective-permute-start(f32[6,66,1,128]{3,1,2,0:T(8,128)S(1)} %copy.29), channel_id=1, source_target_pairs={{0,1},{1,2},{2,3},{4,5},{5,6},{6,7},{8,9},{9,10},{10,11},{12,13},{... | collective-permute-start | bytes 608264 | tf_op jit(solution)/shard_map/ppermute | solution.py:14
where the time goes:
time: 362 us; the launch traced here: 361 us
  other arithmetic  181 us (50%)
  waiting for transfers between devices  86.4 us (24%)
  starting transfers between devices  54.4 us (15%)
  local copies, waits for them, and re-layouts  39.2 us (11%)
    add x4, other arithmetic, advance(): return middle + 0.1 * spread + 0.2 * middle * (1.0 - middle * crowding)  177 us
    ppermute x12, waiting for transfers between devices, with_halo(): lax.ppermute(lax.slice_in_dim(block, 0, width, axis=dim), axis, backward)  49.3 us
    ppermute x12, starting transfers between devices, with_halo(): lax.ppermute(lax.slice_in_dim(block, block.shape[dim] - width, None, axis...  38.3 us
    ppermute x12, waiting for transfers between devices, with_halo(): lax.ppermute(lax.slice_in_dim(block, block.shape[dim] - width, None, axis...  37.1 us
    ppermute x12, starting transfers between devices, with_halo(): lax.ppermute(lax.slice_in_dim(block, 0, width, axis=dim), axis, backward)  16.1 us
    unnamed x24, local copies, waits for them, and re-layouts  13.5 us
    slice x8, local copies, waits for them, and re-layouts, with_halo(): lax.slice_in_dim(block, block.shape[dim] - width, None, axis=dim)  11.6 us
  transfers between devices with their start and end apart: 24, of which 23 were waited for; matrix products, arithmetic and copies ran while one was open for 4% of the time, Pallas kernels for 0%

commit v1 on v0

v1 whole, which is shorter than its diff:
```python
import functools

import jax
import jax.numpy as jnp
from jax import lax
from jax.experimental import pallas as pl
from jax.experimental.pallas import tpu as pltpu
from jax.sharding import PartitionSpec as P

STEPS = 4
EDGE = 4
MIDDLE = 8
PAD = 8
MESH = pl.DeviceIdType.MESH
AXES = ("rows", "cols", "slabs")


def kernel(sizes, chunks, tracer, crowding, out, field, limit, load_sem, store_sem,
           y_send, y_recv, z_send, z_recv, x_send, x_recv):
    rows, width, depth, species = tracer.shape
    last = chunks - 1
    place = {axis: lax.axis_index(axis) for axis in AXES}
    has = {(axis, side): (place[axis] > 0) if side == 0 else (place[axis] < sizes[axis] - 1)
           for axis in AXES for side in (0, 1)}
    near = {(axis, side): {axis: jnp.clip(place[axis] + 2 * side - 1, 0, sizes[axis] - 1)}
            for axis in AXES for side in (0, 1)}

    def span(k):
        if isinstance(k, int):
            if k == 0:
                return 0, EDGE
            if k == last:
                return width - EDGE, EDGE
        return EDGE + (k - 1) * MIDDLE, MIDDLE

    def face(axis, side, p, k, from_input, to):
        start, count = span(k)
        at, cells = pl.ds(PAD, depth), pl.ds(1 + start, count)
        other = 1 - side
        if axis == "rows":
            src = (tracer.at[side * (rows - 1), pl.ds(start, count)] if from_input
                   else field.at[p, 1 + side * (rows - 1), cells, at])
            dst = field.at[p, other * (rows + 1), cells, at]
            send, recv = y_send.at[p, side, k], y_recv.at[p, other, k]
        elif axis == "slabs":
            src = (tracer.at[:, pl.ds(start, count), pl.ds(side * (depth - 1), 1)] if from_input
                   else field.at[p, pl.ds(1, rows), cells, pl.ds(PAD + side * (depth - 1), 1)])
            dst = field.at[p, pl.ds(1, rows), cells, pl.ds(PAD - 1 + other * (depth + 1), 1)]
            send, recv = z_send.at[p, side, k], z_recv.at[p, other, k]
        else:
            src = (tracer.at[:, side * (width - 1)] if from_input
                   else field.at[p, pl.ds(1, rows), 1 + side * (width - 1), at])
            dst = field.at[p, pl.ds(1, rows), other * (width + 1), at]
            send, recv = x_send.at[p, side], x_recv.at[p, other]
        return pltpu.make_async_remote_copy(
            src_ref=src, dst_ref=dst, send_sem=send, recv_sem=recv,
            device_id=near[axis, to], device_id_type=MESH)

    def each(axes, action):
        for axis in axes:
            for side in (0, 1):
                pl.when(has[axis, side])(functools.partial(action, axis, side))

    def send(axes, p, k, from_input=False):
        each(axes, lambda axis, side: face(axis, side, p, k, from_input, side).start())

    def sent(axes, p, k):
        each(axes, lambda axis, side: face(axis, side, p, k, False, side).wait_send())

    def received(axes, p, k):
        each(axes, lambda axis, side: face(axis, 1 - side, p, k, False, side).wait_recv())

    def load(which, k):
        start, count = span(k)
        if which == 0:
            return pltpu.make_async_copy(
                tracer.at[:, pl.ds(start, count)],
                field.at[0, pl.ds(1, rows), pl.ds(1 + start, count), pl.ds(PAD, depth)],
                load_sem.at[0, k])
        return pltpu.make_async_copy(
            crowding.at[:, pl.ds(start, count)], limit.at[:, pl.ds(start, count)], load_sem.at[1, k])

    def store(p, k):
        start, count = span(k)
        return pltpu.make_async_copy(
            field.at[p, pl.ds(1, rows), pl.ds(1 + start, count), pl.ds(PAD, depth)],
            out.at[:, pl.ds(start, count)], store_sem.at[k])

    barrier = pltpu.get_barrier_semaphore()
    each(AXES, lambda axis, side: pl.semaphore_signal(
        barrier, inc=1, device_id=near[axis, side], device_id_type=MESH))
    for k in range(chunks):
        load(0, k).start()
        load(1, k).start()
    pl.semaphore_wait(barrier, sum(jnp.where(has[key], 1, 0) for key in has))

    send(("cols",), 0, 0, True)
    for k in [*range(1, last), 0, last]:
        send(("rows", "slabs"), 0, k, True)

    def clear(axis, side):
        @pl.when(jnp.logical_not(has[axis, side]))
        def _():
            for p in (0, 1):
                if axis == "rows":
                    @pl.loop(1, width + 1)
                    def _(x):
                        field[p, side * (rows + 1), x, pl.ds(PAD, depth)] = jnp.zeros((depth, species), jnp.float32)
                elif axis == "cols":
                    @pl.loop(1, rows + 1)
                    def _(y):
                        field[p, y, side * (width + 1), pl.ds(PAD, depth)] = jnp.zeros((depth, species), jnp.float32)
                else:
                    @pl.loop(1, width + 1)
                    def _(x):
                        for y in range(1, rows + 1):
                            field[p, y, x, pl.ds(PAD - 1 + side * (depth + 1), 1)] = jnp.zeros((1, species), jnp.float32)

    for axis in AXES:
        for side in (0, 1):
            clear(axis, side)

    def advance(step, k):
        p = step % 2
        start, count = span(k)
        scale = 0.2 if step == 0 else 0.05 if step == STEPS - 1 else 0.1

        @pl.loop(0, depth // 8)
        def _(tile):
            at = pl.multiple_of(PAD + tile * 8, 8)
            source = pl.multiple_of(tile * 8, 8)

            def cell(y, x, shift=0):
                return field[p, y, 1 + start + x, pl.ds(at + shift, 8)]

            before = [cell(y, -1) for y in range(1, rows + 1)]
            here = [cell(y, 0) for y in range(1, rows + 1)]
            for x in range(count):
                after = [cell(y, x + 1) for y in range(1, rows + 1)]
                column = [cell(0, x), *here, cell(rows + 1, x)]
                for y in range(rows):
                    middle = here[y]
                    around = (before[y] + after[y]) + (column[y] + column[y + 2])
                    around = around + (cell(y + 1, x, -1) + cell(y + 1, x, 1))
                    bound = limit[y, start + x, pl.ds(source, 8)]
                    if step == 0:
                        bound = bound + bound
                    field[1 - p, y + 1, 1 + start + x, pl.ds(at, 8)] = scale * (around + middle * (6.0 - bound * middle))
                before, here = here, after

    def chunk(step, k, edge):
        p = step % 2
        axes = AXES if edge else ("rows", "slabs")
        if step == 0:
            load(1, k).wait()
            if not edge:
                pl.when(k < last - 1)(lambda: load(0, k + 1).wait())
                pl.when(k == last - 1)(lambda: load(0, last).wait())
        both = ("rows", "slabs")
        received(both, p, k)
        if step >= 1:
            sent(both, 1 - p, k)
        if edge:
            side = 0 if k == 0 else 1
            one = lambda action: pl.when(has["cols", side])(action)
            one(lambda: face("cols", 1 - side, p, k, False, side).wait_recv())
            if step >= 1:
                one(lambda: face("cols", side, 1 - p, k, False, side).wait_send())
        advance(step, k)
        if step < STEPS - 1:
            if edge:
                one(lambda: face("cols", side, 1 - p, k, False, side).start())
            send(both, 1 - p, k)
        else:
            store(1 - p, k).start()

    for step in range(STEPS):
        if step == 0:
            load(0, 0).wait()
            load(0, 1).wait()

        @pl.loop(1, last)
        def _(k):
            chunk(step, k, False)

        chunk(step, 0, True)
        chunk(step, last, True)

    p = (STEPS - 1) % 2

    @pl.loop(1, last)
    def _(k):
        sent(("rows", "slabs"), p, k)
        store(1 - p, k).wait()

    for k in (0, last):
        sent(("rows", "slabs"), p, k)
        store(1 - p, k).wait()
    sent(("cols",), p, 0)


def solution(mesh):
    sizes = dict(mesh.shape)

    def on_device(tracer, crowding):
        rows, width, depth, species = tracer.shape
        chunks = (width - 2 * EDGE) // MIDDLE + 2
        dma = pltpu.SemaphoreType.DMA
        return pl.pallas_call(
            functools.partial(kernel, sizes, chunks),
            out_shape=jax.ShapeDtypeStruct(tracer.shape, jnp.float32),
            in_specs=[pl.BlockSpec(memory_space=pl.ANY)] * 2,
            out_specs=pl.BlockSpec(memory_space=pl.ANY),
            scratch_shapes=[
                pltpu.VMEM((2, rows + 2, width + 2, depth + 2 * PAD, species), jnp.float32),
                pltpu.VMEM(tracer.shape, jnp.float32),
                dma((2, chunks)), dma((chunks,)),
                dma((2, 2, chunks)), dma((2, 2, chunks)),
                dma((2, 2, chunks)), dma((2, 2, chunks)),
                dma((2, 2)), dma((2, 2)),
            ],
            compiler_params=pltpu.CompilerParams(
                collective_id=0, has_side_effects=True, vmem_limit_bytes=67043328),
        )(tracer, crowding)

    return jax.shard_map(
        on_device, mesh=mesh,
        in_specs=(P("rows", "cols", "slabs", None), P("rows", "cols", "slabs", None)),
        out_specs=P("rows", "cols", "slabs", None), check_vma=False)
```

time: 362 us -> 52.3 us (0.14)
  the two profiles are of different devices: /device:TPU:0 before, /device:TPU:30 now
where the time goes in v1:
time: 52.3 us; the launch traced here: 52.1 us
  Pallas kernels  41.5 us (79%)
  local copies, waits for them, and re-layouts  10.6 us (20%)
    pallas_call x1, Pallas kernels, on_device(): pl.pallas_call(functools.partial(kernel, sizes, chunks), out_shape=jax.Sh...  41.5 us
    unnamed x1, local copies, waits for them, and re-layouts  10.6 us

profile of v1, /device:TPU:30, one launch (start us, length us, event | category | flops | bytes accessed | tf_op | source)
XLA Modules:
  0.0 52.1 jit_solution(9645744851343455517)
XLA Ops:
  0.0 41.5 %shard_map.28 = f32[4,64,96,128]{3,2,1,0:T(8,128)} custom-call(f32[4,64,96,128]{3,2,1,0:T(8,128)} %tracer.1, f32[4,64,96,128]{3,2,1,0:T(8,128)} %crowding.1), custom_call_target="tpu_custom_call" | custom-call | tf_op jit(solution)/shard_map/pallas_call | solution.py:209
  41.5 10.6 %copy.4 = f32[4,64,96,128]{3,2,1,0:T(8,128)} copy(f32[4,64,96,128]{3,2,1,0:T(8,128)} %shard_map.28) | data formatting | bytes 25165824

commit v2 on v1

--- a/solution.py
+++ b/solution.py
@@ -11,14 +11,39 @@
 EDGE = 4
 MIDDLE = 8
 PAD = 8
+VMEM_LIMIT = 40 * 1024 * 1024
 MESH = pl.DeviceIdType.MESH
 AXES = ("rows", "cols", "slabs")
 
 
-def kernel(sizes, chunks, tracer, crowding, out, field, limit, load_sem, store_sem,
+class Levels:
+    def __init__(self, *refs):
+        self.refs = refs
+
+    @property
+    def at(self):
+        return self
+
+    def __getitem__(self, index):
+        return self.refs[index[0]].at[index[1:]]
+
+
+def write(ended, out, store_sem):
+    rows, width, depth, species = out.shape
+    copies = [pltpu.make_async_copy(
+        ended.at[1 + y, pl.ds(1, width), pl.ds(PAD, depth)], out.at[y], store_sem.at[y])
+        for y in range(rows)]
+    for copy in copies:
+        copy.start()
+    for copy in copies:
+        copy.wait()
+
+
+def kernel(sizes, chunks, tracer, crowding, ended, other_field, limit, load_sem,
            y_send, y_recv, z_send, z_recv, x_send, x_recv):
     rows, width, depth, species = tracer.shape
     last = chunks - 1
+    field = Levels(ended, other_field)
     place = {axis: lax.axis_index(axis) for axis in AXES}
     has = {(axis, side): (place[axis] > 0) if side == 0 else (place[axis] < sizes[axis] - 1)
            for axis in AXES for side in (0, 1)}
@@ -80,12 +105,6 @@
         return pltpu.make_async_copy(
             crowding.at[:, pl.ds(start, count)], limit.at[:, pl.ds(start, count)], load_sem.at[1, k])
 
-    def store(p, k):
-        start, count = span(k)
-        return pltpu.make_async_copy(
-            field.at[p, pl.ds(1, rows), pl.ds(1 + start, count), pl.ds(PAD, depth)],
-            out.at[:, pl.ds(start, count)], store_sem.at[k])
-
     barrier = pltpu.get_barrier_semaphore()
     each(AXES, lambda axis, side: pl.semaphore_signal(
         barrier, inc=1, device_id=near[axis, side], device_id_type=MESH))
@@ -105,16 +124,16 @@
                 if axis == "rows":
                     @pl.loop(1, width + 1)
                     def _(x):
-                        field[p, side * (rows + 1), x, pl.ds(PAD, depth)] = jnp.zeros((depth, species), jnp.float32)
+                        field.refs[p][side * (rows + 1), x, pl.ds(PAD, depth)] = jnp.zeros((depth, species), jnp.float32)
                 elif axis == "cols":
                     @pl.loop(1, rows + 1)
                     def _(y):
-                        field[p, y, side * (width + 1), pl.ds(PAD, depth)] = jnp.zeros((depth, species), jnp.float32)
+                        field.refs[p][y, side * (width + 1), pl.ds(PAD, depth)] = jnp.zeros((depth, species), jnp.float32)
                 else:
                     @pl.loop(1, width + 1)
                     def _(x):
                         for y in range(1, rows + 1):
-                            field[p, y, x, pl.ds(PAD - 1 + side * (depth + 1), 1)] = jnp.zeros((1, species), jnp.float32)
+                            field.refs[p][y, x, pl.ds(PAD - 1 + side * (depth + 1), 1)] = jnp.zeros((1, species), jnp.float32)
 
     for axis in AXES:
         for side in (0, 1):
@@ -131,7 +150,7 @@
             source = pl.multiple_of(tile * 8, 8)
 
             def cell(y, x, shift=0):
-                return field[p, y, 1 + start + x, pl.ds(at + shift, 8)]
+                return field.refs[p][y, 1 + start + x, pl.ds(at + shift, 8)]
 
             before = [cell(y, -1) for y in range(1, rows + 1)]
             here = [cell(y, 0) for y in range(1, rows + 1)]
@@ -145,7 +164,7 @@
                     bound = limit[y, start + x, pl.ds(source, 8)]
                     if step == 0:
                         bound = bound + bound
-                    field[1 - p, y + 1, 1 + start + x, pl.ds(at, 8)] = scale * (around + middle * (6.0 - bound * middle))
+                    field.refs[1 - p][y + 1, 1 + start + x, pl.ds(at, 8)] = scale * (around + middle * (6.0 - bound * middle))
                 before, here = here, after
 
     def chunk(step, k, edge):
@@ -171,8 +190,6 @@
             if edge:
                 one(lambda: face("cols", side, 1 - p, k, False, side).start())
             send(both, 1 - p, k)
-        else:
-            store(1 - p, k).start()
 
     for step in range(STEPS):
         if step == 0:
@@ -191,11 +208,9 @@
     @pl.loop(1, last)
     def _(k):
         sent(("rows", "slabs"), p, k)
-        store(1 - p, k).wait()
 
     for k in (0, last):
         sent(("rows", "slabs"), p, k)
-        store(1 - p, k).wait()
     sent(("cols",), p, 0)
 
 
@@ -206,22 +221,32 @@
         rows, width, depth, species = tracer.shape
         chunks = (width - 2 * EDGE) // MIDDLE + 2
         dma = pltpu.SemaphoreType.DMA
-        return pl.pallas_call(
+        padded = (rows + 2, width + 2, depth + 2 * PAD, species)
+        cell_count = rows * width * depth * species
+        ended = pl.pallas_call(
             functools.partial(kernel, sizes, chunks),
-            out_shape=jax.ShapeDtypeStruct(tracer.shape, jnp.float32),
+            out_shape=pltpu.VMEM(padded, jnp.float32),
             in_specs=[pl.BlockSpec(memory_space=pl.ANY)] * 2,
-            out_specs=pl.BlockSpec(memory_space=pl.ANY),
+            out_specs=pl.BlockSpec(memory_space=pltpu.VMEM),
             scratch_shapes=[
-                pltpu.VMEM((2, rows + 2, width + 2, depth + 2 * PAD, species), jnp.float32),
+                pltpu.VMEM(padded, jnp.float32),
                 pltpu.VMEM(tracer.shape, jnp.float32),
-                dma((2, chunks)), dma((chunks,)),
+                dma((2, chunks)),
                 dma((2, 2, chunks)), dma((2, 2, chunks)),
                 dma((2, 2, chunks)), dma((2, 2, chunks)),
                 dma((2, 2)), dma((2, 2)),
             ],
             compiler_params=pltpu.CompilerParams(
-                collective_id=0, has_side_effects=True, vmem_limit_bytes=67043328),
+                collective_id=0, has_side_effects=True, vmem_limit_bytes=VMEM_LIMIT),
         )(tracer, crowding)
+        return pl.pallas_call(
+            write,
+            out_shape=jax.ShapeDtypeStruct(tracer.shape, jnp.float32),
+            in_specs=[pl.BlockSpec(memory_space=pltpu.VMEM)],
+            out_specs=pl.BlockSpec(memory_space=pl.ANY),
+            scratch_shapes=[dma((rows,))],
+            compiler_params=pltpu.CompilerParams(vmem_limit_bytes=1 << 20),
+        )(ended)
 
     return jax.shard_map(
         on_device, mesh=mesh,

time: 52.3 us -> 45.5 us (0.87)
  local copies, waits for them, and re-layouts: 10.6 us -> 0 us
  Pallas kernels: 41.5 us -> 45.3 us
    unnamed x1 -> x0, local copies, waits for them, and re-layouts: 10.6 us -> none
    pallas_call x1 -> x2, Pallas kernels: 41.5 us -> 45.3 us  [the longest x1 40.6 us: on_device(): pl.pallas_call(functools.partial(kernel, sizes, chunks), out_shape=pltpu....]
where the time goes in v2:
time: 45.5 us; the launch traced here: 45.3 us
  Pallas kernels  45.3 us (100%)
    pallas_call x1, Pallas kernels, on_device(): pl.pallas_call(functools.partial(kernel, sizes, chunks), out_shape=pltpu....  40.6 us
    pallas_call x1, Pallas kernels, on_device(): pl.pallas_call(write, out_shape=jax.ShapeDtypeStruct(tracer.shape, jnp.fl...  4.72 us

profile of v2, /device:TPU:30, one launch (start us, length us, event | category | flops | bytes accessed | tf_op | source)
XLA Modules:
  0.0 45.3 jit_solution(8549624038294090835)
XLA Ops:
  0.0 40.6 %shard_map.28.ended = f32[6,66,112,128]{3,2,1,0:T(8,128)S(1)} custom-call(f32[4,64,96,128]{3,2,1,0:T(8,128)} %tracer.1, f32[4,64,96,128]{3,2,1,0:T(8,128)} %crowding.1), custom_call_target="tpu_custom_call" | custom-call | tf_op jit(solution)/shard_map/pallas_call | solution.py:226
  40.6 4.7 %shard_map.29 = f32[4,64,96,128]{3,2,1,0:T(8,128)} custom-call(f32[6,66,112,128]{3,2,1,0:T(8,128)S(1)} %shard_map.28.ended), custom_call_target="tpu_custom_call" | custom-call | tf_op jit(solution)/shard_map/pallas_call | solution.py:242

commit v3 on v2

--- a/solution.py
+++ b/solution.py
@@ -8,8 +8,12 @@
 from jax.sharding import PartitionSpec as P
 
 STEPS = 4
-EDGE = 4
-MIDDLE = 8
+EDGE = 2
+VIA = {1: 3, 2: 0}
+GAP = 1
+LATE = 3
+RELAYED = 1
+MIDDLE = 10
 PAD = 8
 VMEM_LIMIT = 40 * 1024 * 1024
 MESH = pl.DeviceIdType.MESH
@@ -39,8 +43,9 @@
         copy.wait()
 
 
-def kernel(sizes, chunks, tracer, crowding, ended, other_field, limit, load_sem,
-           y_send, y_recv, z_send, z_recv, x_send, x_recv):
+def kernel(sizes, chunks, via, tracer, crowding, ended, other_field, limit, load_sem,
+           y_send, y_recv, z_send, z_recv, x_send, x_recv,
+           relayed, r_send, r_recv, f_send, f_recv):
     rows, width, depth, species = tracer.shape
     last = chunks - 1
     field = Levels(ended, other_field)
@@ -50,6 +55,9 @@
     near = {(axis, side): {axis: jnp.clip(place[axis] + 2 * side - 1, 0, sizes[axis] - 1)}
             for axis in AXES for side in (0, 1)}
 
+    col = place["cols"]
+    direct = rows - min(RELAYED, rows // 2) if via else rows
+
     def span(k):
         if isinstance(k, int):
             if k == 0:
@@ -58,7 +66,7 @@
                 return width - EDGE, EDGE
         return EDGE + (k - 1) * MIDDLE, MIDDLE
 
-    def face(axis, side, p, k, from_input, to):
+    def face(axis, side, p, k, from_input, to, part=rows):
         start, count = span(k)
         at, cells = pl.ds(PAD, depth), pl.ds(1 + start, count)
         other = 1 - side
@@ -73,13 +81,65 @@
             dst = field.at[p, pl.ds(1, rows), cells, pl.ds(PAD - 1 + other * (depth + 1), 1)]
             send, recv = z_send.at[p, side, k], z_recv.at[p, other, k]
         else:
-            src = (tracer.at[:, side * (width - 1)] if from_input
-                   else field.at[p, pl.ds(1, rows), 1 + side * (width - 1), at])
-            dst = field.at[p, pl.ds(1, rows), other * (width + 1), at]
+            src = (tracer.at[pl.ds(0, part), side * (width - 1)] if from_input
+                   else field.at[p, pl.ds(1, part), 1 + side * (width - 1), at])
+            dst = field.at[p, pl.ds(1, part), other * (width + 1), at]
             send, recv = x_send.at[p, side], x_recv.at[p, other]
         return pltpu.make_async_remote_copy(
             src_ref=src, dst_ref=dst, send_sem=send, recv_sem=recv,
             device_id=near[axis, to], device_id_type=MESH)
+
+    def x_face(side, to, p, from_input, action):
+        if not via:
+            pl.when(has["cols", to])(lambda: action(face("cols", side, p, 0, from_input, to)))
+            return
+        long = col == 2 - to
+        pl.when(long)(lambda: action(face("cols", side, p, 0, from_input, to, direct)))
+        pl.when(jnp.logical_and(has["cols", to], jnp.logical_not(long)))(
+            lambda: action(face("cols", side, p, 0, from_input, to)))
+
+    def first_hop(source, event, row, from_input):
+        side = 2 - source
+        src = (tracer.at[direct + row, side * (width - 1)] if from_input
+               else field.at[event % 2, 1 + direct + row, 1 + side * (width - 1), pl.ds(PAD, depth)])
+        return pltpu.make_async_remote_copy(
+            src_ref=src, dst_ref=relayed.at[event, row],
+            send_sem=r_send.at[event, row], recv_sem=r_recv.at[event, row],
+            device_id={"cols": via[source]}, device_id_type=MESH)
+
+    def second_hop(source, event, row):
+        side = 2 - source
+        return pltpu.make_async_remote_copy(
+            src_ref=relayed.at[event, row],
+            dst_ref=field.at[event % 2, 1 + direct + row, (1 - side) * (width + 1), pl.ds(PAD, depth)],
+            send_sem=f_send.at[event, row], recv_sem=f_recv.at[event, row],
+            device_id={"cols": 3 - source}, device_id_type=MESH)
+
+    def hops(action, *who):
+        if via:
+            for source in (1, 2):
+                @pl.when(col == who[source - 1])
+                def _():
+                    for row in range(rows - direct):
+                        action(source, row)
+
+    def in_order(action):
+        def both(*sides):
+            for side in sides:
+                action(side)
+
+        if via:
+            pl.when(col == 1)(lambda: both(1, 0))
+            pl.when(col != 1)(lambda: both(0, 1))
+        else:
+            both(0, 1)
+
+    def pass_on(event, row):
+        for source in (1, 2):
+            @pl.when(col == via[source])
+            def _():
+                first_hop(source, event, row, False).wait_recv()
+                second_hop(source, event, row).start()
 
     def each(axes, action):
         for axis in axes:
@@ -111,9 +171,12 @@
     for k in range(chunks):
         load(0, k).start()
         load(1, k).start()
-    pl.semaphore_wait(barrier, sum(jnp.where(has[key], 1, 0) for key in has))
-
-    send(("cols",), 0, 0, True)
+    if via:
+        pl.semaphore_signal(barrier, inc=1, device_id={"cols": lax.rem(col + 2, 4)}, device_id_type=MESH)
+    pl.semaphore_wait(barrier, (1 if via else 0) + sum(jnp.where(has[key], 1, 0) for key in has))
+
+    hops(lambda source, row: first_hop(source, 0, row, True).start(), 1, 2)
+    in_order(lambda side: x_face(side, side, 0, True, lambda copy: copy.start()))
     for k in [*range(1, last), 0, last]:
         send(("rows", "slabs"), 0, k, True)
 
@@ -181,14 +244,28 @@
             sent(both, 1 - p, k)
         if edge:
             side = 0 if k == 0 else 1
-            one = lambda action: pl.when(has["cols", side])(action)
-            one(lambda: face("cols", 1 - side, p, k, False, side).wait_recv())
+            x_face(1 - side, side, p, False, lambda copy: copy.wait_recv())
+            if via:
+                @pl.when(col == 2 - side)
+                def _():
+                    for row in range(rows - direct):
+                        second_hop(1 + side, step, row).wait_recv()
             if step >= 1:
-                one(lambda: face("cols", side, 1 - p, k, False, side).wait_send())
+                x_face(side, side, 1 - p, False, lambda copy: copy.wait_send())
+                if via:
+                    @pl.when(col == 2 - side)
+                    def _():
+                        for row in range(rows - direct):
+                            first_hop(2 - side, step - 1, row, False).wait_send()
         advance(step, k)
         if step < STEPS - 1:
             if edge:
-                one(lambda: face("cols", side, 1 - p, k, False, side).start())
+                if via:
+                    @pl.when(col == 2 - side)
+                    def _():
+                        for row in range(rows - direct):
+                            first_hop(2 - side, step + 1, row, False).start()
+                x_face(side, side, 1 - p, False, lambda copy: copy.start())
             send(both, 1 - p, k)
 
     for step in range(STEPS):
@@ -199,9 +276,12 @@
         @pl.loop(1, last)
         def _(k):
             chunk(step, k, False)
-
-        chunk(step, 0, True)
-        chunk(step, last, True)
+            if via:
+                for row in range(rows - direct):
+                    pl.when(k == max(1, last - 1 - LATE - GAP * (rows - direct - 1 - row)))(
+                        functools.partial(pass_on, step, row))
+
+        in_order(lambda side: chunk(step, side * last, True))
 
     p = (STEPS - 1) % 2
 
@@ -211,11 +291,27 @@
 
     for k in (0, last):
         sent(("rows", "slabs"), p, k)
-    sent(("cols",), p, 0)
+    for side in (0, 1):
+        x_face(side, side, p, False, lambda copy: copy.wait_send())
+    hops(lambda source, row: first_hop(source, STEPS - 1, row, False).wait_send(), 1, 2)
+    for event in range(STEPS):
+        hops(lambda source, row: second_hop(source, event, row).wait_send(), *[via[k] for k in (1, 2)] if via else ())
+
+
+def relays(mesh):
+    if mesh.shape["cols"] != 4:
+        return None
+    devices = mesh.devices.transpose([mesh.axis_names.index(axis) for axis in AXES])[0, :, 0]
+    chips = [getattr(device, "coords", None) for device in devices]
+    if any(chip is None for chip in chips):
+        return None
+    apart = sum(a != b for a, b in zip(chips[1], chips[2]))
+    return VIA if apart > 1 else None
 
 
 def solution(mesh):
     sizes = dict(mesh.shape)
+    via = relays(mesh)
 
     def on_device(tracer, crowding):
         rows, width, depth, species = tracer.shape
@@ -224,7 +320,7 @@
         padded = (rows + 2, width + 2, depth + 2 * PAD, species)
         cell_count = rows * width * depth * species
         ended = pl.pallas_call(
-            functools.partial(kernel, sizes, chunks),
+            functools.partial(kernel, sizes, chunks, via),
             out_shape=pltpu.VMEM(padded, jnp.float32),
             in_specs=[pl.BlockSpec(memory_space=pl.ANY)] * 2,
             out_specs=pl.BlockSpec(memory_space=pltpu.VMEM),
@@ -235,6 +331,8 @@
                 dma((2, 2, chunks)), dma((2, 2, chunks)),
                 dma((2, 2, chunks)), dma((2, 2, chunks)),
                 dma((2, 2)), dma((2, 2)),
+                pltpu.VMEM((STEPS, max(1, rows // 2), depth, species), jnp.float32),
+                *[dma((STEPS, max(1, rows // 2)))] * 4,
             ],
             compiler_params=pltpu.CompilerParams(
                 collective_id=0, has_side_effects=True, vmem_limit_bytes=VMEM_LIMIT),

time: 45.5 us -> 42.3 us (0.930)
  the two profiles are of different devices: /device:TPU:30 before, /device:TPU:0 now
where the time goes in v3:
time: 42.3 us; the launch traced here: 42.1 us
  Pallas kernels  42.1 us (100%)
    pallas_call x1, Pallas kernels, on_device(): pl.pallas_call(functools.partial(kernel, sizes, chunks, via), out_shape=p...  37.4 us
    pallas_call x1, Pallas kernels, on_device(): pl.pallas_call(write, out_shape=jax.ShapeDtypeStruct(tracer.shape, jnp.fl...  4.72 us

profile of v3, /device:TPU:0, one launch (start us, length us, event | category | flops | bytes accessed | tf_op | source)
XLA Modules:
  0.0 42.1 jit_solution(4809154029340356588)
XLA Ops:
  0.0 37.4 %shard_map.28.ended = f32[6,66,112,128]{3,2,1,0:T(8,128)S(1)} custom-call(f32[4,64,96,128]{3,2,1,0:T(8,128)} %tracer.1, f32[4,64,96,128]{3,2,1,0:T(8,128)} %crowding.1), custom_call_target="tpu_custom_call" | custom-call | tf_op jit(solution)/shard_map/pallas_call | solution.py:322
  37.4 4.7 %shard_map.29 = f32[4,64,96,128]{3,2,1,0:T(8,128)} custom-call(f32[6,66,112,128]{3,2,1,0:T(8,128)S(1)} %shard_map.28.ended), custom_call_target="tpu_custom_call" | custom-call | tf_op jit(solution)/shard_map/pallas_call | solution.py:340
